TPU v7x, 256 devices: a whole 4x4x8 slice. The times are simulated.
256 devices in a mesh: rows: 256 (over y, x, z, core).
Axes of the slice: x: 4, y: 4, z: 8, core: 2. Of those that a mesh axis runs over, the one named last changes fastest.
Arguments:
- factor: bfloat16 [2097152, 256], P('rows')
- cand_weights: bfloat16 [524288, 1024], P('rows'), may hold values from -2 to 2
- cand_block: int32 [1024], replicated, may hold values from 0 to 3
- noise: float32 [1024], replicated, may hold values from 0.3 to 3
- chosen: int32 [2], replicated, may hold values from 0 to 1023
Outputs:
- scores: float32 [2, 1024], P(None, 'rows')
- updates: float32 [2, 2097152], P(None, 'rows')
All inputs are finite; a program needn't handle non-finite values.
Results may differ from a plain program's by a relative error of at most 0.00055.
Values sent between devices are 32-bit elements; how exact they have to be, the bound alone decides.
No kernel may reach another device: no remote copies, remote signals or barrier semaphores. Data moves between devices by JAX's collectives and lax.ppermute only.
A program may use at most 128 MiB of HBM per device.

v0:
```python
import jax
import jax.numpy as jnp
from jax import lax
from jax.experimental import pallas as pl
from jax.experimental.pallas import tpu as pltpu
from jax.sharding import Mesh
from jax.sharding import PartitionSpec as P

NB = 4
R = 256
NCAND = 1024
LANES = 128
NYX = 16
NZ = 8
SLOTS = NZ + 2
STEPS = 4
ROWS = ("rows_0", "rows_1", "rows_2", "rows_3")
YX = ("rows_0", "rows_1")
HIGHEST = lax.Precision.HIGHEST


def iota(shape, dim):
    return lax.broadcasted_iota(jnp.int32, shape, dim)


def matmul(a, b, dims=((1,), (0,)), precision=None):
    return lax.dot_general(
        a, b, (dims, ((), ())), preferred_element_type=jnp.float32, precision=precision
    )


def local_kernel(
    chosen, blocks, core, fac, wts, block_row, mine, theirs, dense,
    fwide, acc, gram, sq8, cross8, masks, wsel, pay,
):
    step = pl.program_id(0)
    wrows = wts.shape[0]
    first, second = chosen[0], chosen[1]

    @pl.when(step == 0)
    def _():
        acc[...] = jnp.zeros_like(acc)
        gram[...] = jnp.zeros_like(gram)
        sq8[...] = jnp.zeros_like(sq8)
        cross8[...] = jnp.zeros_like(cross8)
        pay[:, :, NZ:, :, :] = jnp.zeros((2, NYX, 2, 8, LANES), jnp.float32)
        column = jnp.broadcast_to(block_row[...], (LANES, NCAND)).T
        for b in range(NB):
            masks[b] = jnp.where(column == float(b), 1.0, 0.0).astype(jnp.bfloat16)

    w = wts[...]
    for h in range(2):
        fwide[h] = fac[:, LANES * h : LANES * (h + 1)].astype(jnp.float32)
    turned = w.T
    total = acc[...]
    gsum = gram[...]
    for b in range(NB):
        fb = jnp.concatenate(
            [fwide[h, pl.ds(b, wrows, stride=NB), :] for h in range(2)], axis=1
        ).astype(jnp.bfloat16)
        mask = masks[b]
        seen = jnp.concatenate(
            [turned[:, LANES * q : LANES * (q + 1)] * mask for q in range(wrows // LANES)], axis=1
        )
        total = total + matmul(seen, fb)
        gsum = gsum + matmul(fb, fb, ((0,), (0,)))
    acc[...] = total
    gram[...] = gsum
    wf = w.astype(jnp.float32)
    sq8[...] += jnp.sum((wf * wf).reshape(wrows // 8, 8, NCAND), axis=0)
    rows = iota((16, LANES), 0)
    lanes = iota((16, LANES), 1)
    picked = jnp.zeros((16, wrows), jnp.float32)
    for row, cand in ((0, first), (1, second)):
        base = pl.multiple_of((cand // LANES) * LANES, LANES)
        hot = jnp.where((rows == row) & (lanes == cand - base), 1.0, 0.0).astype(jnp.bfloat16)
        picked = picked + matmul(hot, wts[:, pl.ds(base, LANES)], ((1,), (1,)))
    cross8[...] += matmul(picked.astype(jnp.bfloat16), w)[:8]
    for q in range(wrows // LANES):
        wsel[step * (wrows // LANES) + q] = picked[:8, LANES * q : LANES * (q + 1)]

    @pl.when(step == STEPS - 1)
    def _():
        proj = acc[...]
        for h in range(2):
            half = proj[:, LANES * h : LANES * (h + 1)]
            pay[h, :, :NZ, :, :] = half.reshape(NYX, NZ, 8, LANES)
        g = gram[...]
        pay[0, :, NZ, :, :] = g[:LANES, :LANES].reshape(NYX, 8, LANES)
        pay[1, :, NZ, :, :] = g[:LANES, LANES:].reshape(NYX, 8, LANES)
        low = g[LANES:, LANES:].reshape(2, NYX // 2, 8, LANES)
        pay[0, : NYX // 2, NZ + 1, :, :] = low[0]
        pay[1, : NYX // 2, NZ + 1, :, :] = low[1]
        for row, cand in ((0, first), (1, second)):
            line = acc[pl.ds(cand, 1), :]
            for h in range(2):
                pay[0, NYX // 2, NZ + 1, 2 * row + h : 2 * row + h + 1, :] = line[
                    :, LANES * h : LANES * (h + 1)
                ]
        sq = jnp.sum(sq8[...], axis=0, keepdims=True)
        same = block_row[...] == blocks[first].astype(jnp.float32)
        cross = jnp.where(same, cross8[0:1, :], 0.0)
        for q in range(NCAND // LANES):
            part = slice(LANES * q, LANES * (q + 1))
            pay[1, NYX // 2, NZ + 1, q : q + 1, :] = sq[:, part]
            pay[1, NYX // 2 + 1, NZ + 1, q : q + 1, :] = cross[:, part]
        mine[...] = pay[core[0]]
        theirs[...] = pay[1 - core[0]]
        wide = LANES * NB
        spread = jnp.where(
            iota((LANES, wide), 0) == iota((LANES, wide), 1) // NB, 1.0, 0.0
        ).astype(jnp.bfloat16)
        groups = wsel.shape[0]
        lines = wsel[...].reshape(groups * 8, LANES).astype(jnp.bfloat16)
        repeated = matmul(lines, spread).reshape(groups, 8, wide)
        row = iota((groups, 8, wide), 1)
        place = iota((groups, 8, wide), 2) % NB
        wanted = jnp.where(row == 0, blocks[first], blocks[second])
        dense[...] = jnp.where(place == wanted, repeated, 0.0)


def local_products(factor, cand_weights, cand_block, chosen, core):
    rows, rank = factor.shape
    wrows = cand_weights.shape[0]
    fstep, wstep = rows // STEPS, wrows // STEPS
    groups = wrows // LANES
    payload = jax.ShapeDtypeStruct((NYX, SLOTS, 8, LANES), jnp.float32)
    fixed4 = pl.BlockSpec((NYX, SLOTS, 8, LANES), lambda i, *_: (0, 0, 0, 0))
    return pl.pallas_call(
        local_kernel,
        grid_spec=pltpu.PrefetchScalarGridSpec(
            num_scalar_prefetch=3,
            grid=(STEPS,),
            in_specs=[
                pl.BlockSpec((fstep, rank), lambda i, *_: (i, 0)),
                pl.BlockSpec((wstep, NCAND), lambda i, *_: (i, 0)),
                pl.BlockSpec((1, NCAND), lambda i, *_: (0, 0)),
            ],
            out_specs=[
                fixed4,
                fixed4,
                pl.BlockSpec((groups, 8, LANES * NB), lambda i, *_: (0, 0, 0)),
            ],
            scratch_shapes=[
                pltpu.VMEM((2, fstep, LANES), jnp.float32),
                pltpu.VMEM((NCAND, rank), jnp.float32),
                pltpu.VMEM((rank, rank), jnp.float32),
                pltpu.VMEM((8, NCAND), jnp.float32),
                pltpu.VMEM((8, NCAND), jnp.float32),
                pltpu.VMEM((NB, NCAND, LANES), jnp.bfloat16),
                pltpu.VMEM((groups, 8, LANES), jnp.float32),
                pltpu.VMEM((2, NYX, SLOTS, 8, LANES), jnp.float32),
            ],
        ),
        out_shape=[payload, payload, jax.ShapeDtypeStruct((groups, 8, LANES * NB), jnp.float32)],
        compiler_params=pltpu.CompilerParams(
            dimension_semantics=("arbitrary",), vmem_limit_bytes=60 * 2**20
        ),
        name="local",
    )(
        chosen,
        cand_block,
        core,
        factor,
        cand_weights,
        cand_block.astype(jnp.float32).reshape(1, NCAND),
    )


def total(x):
    return jnp.sum(jnp.sum(x, axis=1, keepdims=True), axis=0, keepdims=True)


def lane_sum(x):
    return jnp.sum(x, axis=1, keepdims=True)


def finish_kernel(
    chosen, where, gmine, gtheirs, pmine, ptheirs, noise, dense, factor, scores, updates,
    fvmem, m, x, sem,
):
    copy = pltpu.make_async_copy(factor, fvmem, sem)
    copy.start()
    core, chip = where[0], where[1]
    first, second = chosen[0], chosen[1]
    own = core == 0
    a_, b_ = gmine[...], gtheirs[...]
    g0 = jnp.where(own, a_, b_)
    g1 = jnp.where(own, b_, a_)
    half = NYX // 2
    top = g0[:, 0].reshape(LANES, LANES)
    side = g1[:, 0].reshape(LANES, LANES)
    low = jnp.concatenate([g0[:half, 1], g1[:half, 1]], axis=0).reshape(LANES, LANES)
    diag = iota((LANES, LANES), 0) == iota((LANES, LANES), 1)
    m[:LANES, :LANES] = top + jnp.where(diag, 1.0, 0.0)
    m[:LANES, LANES:] = side
    m[LANES:, :LANES] = side.T
    m[LANES:, LANES:] = low + jnp.where(diag, 1.0, 0.0)
    psel, sq, cross = g0[half, 1], g1[half, 1], g1[half + 1, 1]
    p_, q_ = pmine[...], ptheirs[...]
    pown = jnp.concatenate([jnp.where(own, p_, q_), jnp.where(own, q_, p_)], axis=1)
    pj = jnp.concatenate([psel[0:1], psel[1:2]], axis=1)
    pk = jnp.concatenate([psel[2:3], psel[3:4]], axis=1)
    rid = iota((8, R), 0)
    pboth = jnp.where(rid >= 6, 0.0, jnp.where(rid % 2 == 0, pj, pk))
    rhs = jnp.concatenate([pown, pboth], axis=0)

    full = m[...]
    rowmax = jnp.max(jnp.sum(jnp.abs(full), axis=0, keepdims=True))
    bound = jnp.maximum(rowmax, 1.0)
    rho0 = (bound - 1.0) / (bound + 1.0)
    alpha = 2.0 / (bound + 1.0)
    eye = jnp.where(iota((R, R), 0) == iota((R, R), 1), 1.0, 0.0)
    scale0 = 2.0 / (2.0 - rho0 * rho0)
    x[...] = (scale0 * alpha) * (2.0 * eye - alpha * full)
    rho1 = rho0 * rho0 / (2.0 - rho0 * rho0)

    def newton(carry):
        rho, count = carry
        scale = 2.0 / (2.0 - rho * rho)
        now = x[...]
        prod = matmul(m[...], now, precision=HIGHEST)
        x[...] = scale * (2.0 * now - matmul(now, prod, precision=HIGHEST))
        return rho * rho / (2.0 - rho * rho), count + 1

    lax.while_loop(lambda s: (s[0] > 5e-3) & (s[1] < 100), newton, (rho1, jnp.int32(0)))
    inv = x[...]
    a = matmul(rhs, inv, precision=HIGHEST)
    for _ in range(2):
        left = rhs - matmul(a, full, precision=HIGHEST)
        a = a + matmul(left, inv, precision=HIGHEST)

    aown, aboth = a[:8], a[8:]
    aj, ak = aboth[0:1], aboth[1:2]
    rows = iota((8, LANES), 0)
    lanes = iota((8, LANES), 1)
    flat = rows * LANES + lanes
    nz = noise[...]

    def at(tile, cand):
        return total(jnp.where(flat == cand, tile, 0.0))

    def owned(tile):
        line = jnp.sum(jnp.where(rows == chip // NYX, tile, 0.0), axis=0, keepdims=True)
        return lane_sum(jnp.where(lanes == (chip % NYX) * 8 + rows, line, 0.0))

    sqc, crossc, noisec = owned(sq), owned(cross), owned(nz)
    pa = lane_sum(pown * aown)
    aa = lane_sum(aown * aown)
    pja = lane_sum(aown * pj)
    aja = lane_sum(aown * aj)
    q = sqc - pa
    nrm = sqc - 2.0 * pa + (pa - aa)
    paj = lane_sum(pj * aj)
    qj = at(sq, first) - paj
    big = at(sq, first) - 2.0 * paj + (paj - lane_sum(aj * aj))
    d1 = at(nz, first) + qj
    u = crossc - pja
    e = u - aja
    q2 = q - u * u / d1
    nrm2 = nrm - 2.0 * u * e / d1 + u * u * big / (d1 * d1)
    for row, s in ((0, nrm / (noisec + q)), (1, nrm2 / (noisec + q2))):
        line = jnp.sum(jnp.where(rows == lanes + 4 * core, s, 0.0), axis=0, keepdims=True)
        scores[row : row + 1, :] = line[:, :4]
    uk = at(cross, second) - lane_sum(pj * ak)
    qk = at(sq, second) - lane_sum(pk * ak)
    d2 = at(nz, second) + qk - uk * uk / d1
    r1 = 1.0 / jnp.sqrt(d1)
    r2 = 1.0 / jnp.sqrt(d2)
    ratio = uk / d1

    high = aboth.astype(jnp.bfloat16).astype(jnp.float32)
    rest = aboth - high
    mid = rest.astype(jnp.bfloat16).astype(jnp.float32)
    pieces = jnp.where(rid < 2, high, jnp.where(rid < 4, mid, rest - mid)).astype(jnp.bfloat16)
    copy.wait()
    wide = LANES * NB
    for g in range(dense.shape[0]):
        part = slice(wide * g, wide * (g + 1))
        got = matmul(pieces, fvmem[part, :], ((1,), (1,)))
        applied = got[0:2] + got[2:4] + got[4:6]
        left = dense[g][0:2] - applied
        w1 = left[0:1]
        updates[0:1, part] = w1 * r1
        updates[1:2, part] = (left[1:2] - w1 * ratio) * r2


def finish(gmine, gtheirs, pmine, ptheirs, noise, dense, factor, chosen, where):
    local_rows = factor.shape[0]
    vmem = pl.BlockSpec(memory_space=pltpu.VMEM)
    return pl.pallas_call(
        finish_kernel,
        grid_spec=pltpu.PrefetchScalarGridSpec(
            num_scalar_prefetch=2,
            grid=(),
            in_specs=[vmem] * 6 + [pl.BlockSpec(memory_space=pl.ANY)],
            out_specs=[vmem, vmem],
            scratch_shapes=[
                pltpu.VMEM(factor.shape, jnp.bfloat16),
                pltpu.VMEM((R, R), jnp.float32),
                pltpu.VMEM((R, R), jnp.float32),
                pltpu.SemaphoreType.DMA,
            ],
        ),
        out_shape=[
            jax.ShapeDtypeStruct((2, 4), jnp.float32),
            jax.ShapeDtypeStruct((2, local_rows), jnp.float32),
        ],
        compiler_params=pltpu.CompilerParams(vmem_limit_bytes=40 * 2**20),
        name="finish",
    )(chosen, where, gmine, gtheirs, pmine, ptheirs, noise, dense, factor)


def swap_cores(x):
    return lax.ppermute(x, "rows_3", [(0, 1), (1, 0)])


def per_device(factor, cand_weights, cand_block, noise, chosen):
    core = lax.axis_index("rows_3").astype(jnp.int32)
    chip = lax.axis_index(("rows_0", "rows_1", "rows_2")).astype(jnp.int32)
    mine, theirs, dense = local_products(
        factor, cand_weights, cand_block, chosen, core.reshape(1)
    )
    pair = mine + swap_cores(theirs)
    plane = jnp.sum(lax.all_to_all(pair, YX, 0, 0, tiled=True), axis=0)
    shared = jnp.broadcast_to(plane[None, NZ:], (NZ, 2, 8, LANES))
    line = jnp.concatenate([plane[:NZ, None], shared], axis=1)
    summed = jnp.sum(lax.all_to_all(line, "rows_2", 0, 0, tiled=True), axis=0)
    pmine = summed[0]
    ptheirs = swap_cores(pmine)
    copies = jnp.broadcast_to(summed[None, 1:], (NYX, 2, 8, LANES))
    gmine = lax.all_to_all(copies, YX, 0, 0, tiled=True)
    gtheirs = swap_cores(gmine)
    scores, updates = finish(
        gmine, gtheirs, pmine, ptheirs, noise.reshape(8, LANES), dense, factor, chosen,
        jnp.stack([core, chip]),
    )
    return scores, updates


def solution(mesh):
    torus = Mesh(mesh.devices.reshape(4, 4, 8, 2), ROWS)
    return jax.shard_map(
        per_device,
        mesh=torus,
        in_specs=(P(ROWS, None), P(ROWS, None), P(), P(), P()),
        out_specs=(P(None, ROWS), P(None, ROWS)),
        check_vma=False,
    )
```

profile of v0, /device:TPU:1, one launch (start us, length us, event | category | flops | bytes accessed | tf_op | source)
XLA Modules:
  0.0 83.7 jit_solution(11196124899367891798)
XLA Ops:
  0.6 1.3 %convert_element_type.3 = f32[1024]{0:T(1024)} convert(s32[1024]{0:T(1024)} %blocks.1) | non-fusion elementwise | flops 1024 | bytes 8192 | tf_op jit(solution)/shard_map/convert_element_type | solution.py:166
  1.9 11.7 %local.1 = (f32[16,10,8,128]{3,2,1,0:T(8,128)}, f32[16,10,8,128]{3,2,1,0:T(8,128)}, f32[16,8,512]{2,1,0:T(8,128)}) custom-call(s32[2]{0:T(128)} %chosen.3, s32[1024]{0:T(1024)} %blocks.1, s32[1]{0:T(128)} %bitcast.core, bf16[8192,256]{1,0:T(8,128)(2,1)} %factor.1, bf16[2048,1024]{1,0:T(8,128)(2,1)} %wts.1, f32[1,1024]{1,0:T(1,128)} %bitcast.9), custom_call_target="tpu_custom_call" | custom-call | tf_op jit(solution)/shard_map/local/pallas_call | solution.py:129
  13.6 0.0 copy-start.1
  13.6 0.0 copy-start.2
  13.6 0.0 copy-start.3
  13.6 3.3 %collective-permute-start = (f32[16,10,8,128]{3,2,1,0:T(8,128)}, f32[16,10,8,128]{3,2,1,0:T(8,128)S(1)}, u32[]{:S(2)}, u32[]{:S(2)}) collective-permute-start(f32[16,10,8,128]{3,2,1,0:T(8,128)} %get-tuple-element.6), channel_id=1, source_target_pairs={{0,1},{1,0},{2,3},{3,2},{4,5},{5,4},{6,7},{7,6},{8,9},{9,8},{10,11... | collective-permute-start | bytes 1966088 | tf_op jit(solution)/shard_map/ppermute | solution.py:315
  16.9 1.9 %collective-permute-done = f32[16,10,8,128]{3,2,1,0:T(8,128)S(1)} collective-permute-done((f32[16,10,8,128]{3,2,1,0:T(8,128)}, f32[16,10,8,128]{3,2,1,0:T(8,128)S(1)}, u32[]{:S(2)}, u32[]{:S(2)}) %collective-permute-start) | collective-permute-done | bytes 655392 | tf_op jit(solution)/shard_map/ppermute | solution.py:315
  18.8 1.2 %add.11 = f32[16,10,8,128]{3,2,1,0:T(8,128)S(1)} add(f32[16,10,8,128]{3,2,1,0:T(8,128)} %get-tuple-element.5, f32[16,10,8,128]{3,2,1,0:T(8,128)S(1)} %collective-permute-done) | non-fusion elementwise | flops 163840 | bytes 1966080 | tf_op jit(solution)/shard_map/add | solution.py:324
  20.0 17.3 %all_to_all.15 = f32[16,10,8,128]{3,2,1,0:T(8,128)S(1)} all-to-all(f32[16,10,8,128]{3,2,1,0:T(8,128)S(1)} %add.11), channel_id=1, replica_groups=mesh['rows_0'=4,'rows_1'=4,'rows_2'=8,'rows_3'=2] {'rows_0','rows_1'}, dimensions={0} | all-to-all | bytes 1310720 | tf_op jit(solution)/shard_map/all_to_all | solution.py:325
  37.4 15.6 %all_to_all.16 = f32[8,3,8,128]{3,2,1,0:T(8,128)S(1)} all-to-all(f32[8,3,8,128]{3,2,1,0:T(8,128)S(1)} %pad_maximum_fusion), channel_id=1, replica_groups=mesh['rows_0'=4,'rows_1'=4,'rows_2'=8,'rows_3'=2] {'rows_2'}, dimensions={0} | all-to-all | bytes 196608 | tf_op jit(solution)/shard_map/all_to_all | solution.py:328
  53.0 0.7 broadcast_in_dim.8
  53.6 3.5 %all-to-all-start.2 = ((f32[16,2,8,128]{3,2,1,0:T(8,128)}), f32[16,2,8,128]{3,2,1,0:T(8,128)S(1)}, u32[]{:S(2)}, u32[]{:S(2)}) async-start(f32[16,2,8,128]{3,2,1,0:T(8,128)} %broadcast_in_dim.8), calls=%async_computation.2 | async-start | bytes 262144 | tf_op jit(solution)/shard_map/all_to_all | solution.py:332
  57.2 6.8 %all-to-all-done.2.gmine = f32[16,2,8,128]{3,2,1,0:T(8,128)S(1)} async-done(((f32[16,2,8,128]{3,2,1,0:T(8,128)}), f32[16,2,8,128]{3,2,1,0:T(8,128)S(1)}, u32[]{:S(2)}, u32[]{:S(2)}) %all-to-all-start.2) | async-done | bytes 131104 | tf_op jit(solution)/shard_map/all_to_all | solution.py:332
  64.0 4.0 %collective-permute-start.1 = (f32[16,2,8,128]{3,2,1,0:T(8,128)S(1)}, f32[16,2,8,128]{3,2,1,0:T(8,128)S(1)}, u32[]{:S(2)}, u32[]{:S(2)}) collective-permute-start(f32[16,2,8,128]{3,2,1,0:T(8,128)S(1)} %all-to-all-done.2.gmine), channel_id=1, source_target_pairs={{0,1},{1,0},{2,3},{3,2},{4,5},{5,4},{6,7},{7,6},{8,9},{9,8},{10,11... | collective-permute-start | bytes 393224 | tf_op jit(solution)/shard_map/ppermute | solution.py:315
  68.0 0.0 collective-permute-start.2
  68.0 0.1 pad_add_fusion.where
  68.1 1.1 %collective-permute-done.2.ptheirs = f32[8,128]{1,0:T(8,128)S(1)} collective-permute-done((f32[8,128]{1,0:T(8,128)S(1)}, f32[8,128]{1,0:T(8,128)S(1)}, u32[]{:S(2)}, u32[]{:S(2)}) %collective-permute-start.2) | collective-permute-done | bytes 4128 | tf_op jit(solution)/shard_map/ppermute | solution.py:315
  69.2 0.0 collective-permute-done.1.gtheirs
  69.2 0.0 copy-done.1
  69.2 0.0 copy-done.2
  69.2 0.0 copy-done.3
  69.2 0.0 copy-start
  69.2 2.2 %copy-done = bf16[8192,256]{1,0:T(8,128)(2,1)S(1)} copy-done((bf16[8192,256]{1,0:T(8,128)(2,1)S(1)}, bf16[8192,256]{1,0:T(8,128)(2,1)}, u32[]{:S(2)}) %copy-start) | copy-done | bytes 4194328
  71.4 12.3 %finish.1 = (f32[2,4]{1,0:T(2,128)}, f32[2,8192]{1,0:T(2,128)}) custom-call(s32[2]{0:T(128)S(1)} %copy-done.3, s32[2]{0:T(128)S(1)} %pad_add_fusion.where, f32[16,2,8,128]{3,2,1,0:T(8,128)S(1)} %all-to-all-done.2.gmine, f32[16,2,8,128]{3,2,1,0:T(8,128)S(1)} %collective-permute-done.1.gtheirs, f32[8,128]{1,0:T(8,128)S(1)} %slice_bitcast_fusion.1.pmine, ...), custom_call_target="tpu_custom_call" | custom-call | tf_op jit(solution)/shard_map/finish/pallas_call | solution.py:291
  (8 shorter events, 0.1 us)
Async XLA Ops:
  13.6 55.6 %copy-start.1 = (f32[16,8,512]{2,1,0:T(8,128)S(1)}, f32[16,8,512]{2,1,0:T(8,128)}, u32[]{:S(2)}) copy-start(f32[16,8,512]{2,1,0:T(8,128)} %get-tuple-element.7.dense) | copy-start | bytes 786436
  13.6 55.6 %copy-start.2 = (f32[1024]{0:T(1024)S(1)}, f32[1024]{0:T(1024)}, u32[]{:S(2)}) copy-start(f32[1024]{0:T(1024)} %param.8) | copy-start | bytes 12292
  13.6 55.6 %copy-start.3 = (s32[2]{0:T(128)S(1)}, s32[2]{0:T(128)}, u32[]{:S(2)}) copy-start(s32[2]{0:T(128)} %chosen.3) | copy-start | bytes 28
  13.6 5.2 %collective-permute-start = (f32[16,10,8,128]{3,2,1,0:T(8,128)}, f32[16,10,8,128]{3,2,1,0:T(8,128)S(1)}, u32[]{:S(2)}, u32[]{:S(2)}) collective-permute-start(f32[16,10,8,128]{3,2,1,0:T(8,128)} %get-tuple-element.6), channel_id=1, source_target_pairs={{0,1},{1,0},{2,3},{3,2},{4,5},{5,4},{6,7},{7,6},{8,9},{9,8},{10,11... | collective-permute-start | bytes 1966088 | tf_op jit(solution)/shard_map/ppermute | solution.py:315
  53.6 10.3 %all-to-all-start.2 = ((f32[16,2,8,128]{3,2,1,0:T(8,128)}), f32[16,2,8,128]{3,2,1,0:T(8,128)S(1)}, u32[]{:S(2)}, u32[]{:S(2)}) async-start(f32[16,2,8,128]{3,2,1,0:T(8,128)} %broadcast_in_dim.8), calls=%async_computation.2 | async-start | bytes 262144 | tf_op jit(solution)/shard_map/all_to_all | solution.py:332
  64.0 5.2 %collective-permute-start.1 = (f32[16,2,8,128]{3,2,1,0:T(8,128)S(1)}, f32[16,2,8,128]{3,2,1,0:T(8,128)S(1)}, u32[]{:S(2)}, u32[]{:S(2)}) collective-permute-start(f32[16,2,8,128]{3,2,1,0:T(8,128)S(1)} %all-to-all-done.2.gmine), channel_id=1, source_target_pairs={{0,1},{1,0},{2,3},{3,2},{4,5},{5,4},{6,7},{7,6},{8,9},{9,8},{10,11... | collective-permute-start | bytes 393224 | tf_op jit(solution)/shard_map/ppermute | solution.py:315
  68.0 1.2 %collective-permute-start.2 = (f32[8,128]{1,0:T(8,128)S(1)}, f32[8,128]{1,0:T(8,128)S(1)}, u32[]{:S(2)}, u32[]{:S(2)}) collective-permute-start(f32[8,128]{1,0:T(8,128)S(1)} %slice_bitcast_fusion.1.pmine), channel_id=1, source_target_pairs={{0,1},{1,0},{2,3},{3,2},{4,5},{5,4},{6,7},{7,6},{8,9},{9,8},{10,11... | collective-permute-start | bytes 12296 | tf_op jit(solution)/shard_map/ppermute | solution.py:315
  69.2 2.2 %copy-start = (bf16[8192,256]{1,0:T(8,128)(2,1)S(1)}, bf16[8192,256]{1,0:T(8,128)(2,1)}, u32[]{:S(2)}) copy-start(bf16[8192,256]{1,0:T(8,128)(2,1)} %factor.1) | copy-start | bytes 12582916
where the time goes:
time: 84.1 us; the launch traced here: 83.7 us
  blocking collectives  32.8 us (39%)
  Pallas kernels  24 us (29%)
  starting transfers between devices  10.8 us (13%)
  waiting for transfers between devices  9.82 us (12%)
  local copies, waits for them, and re-layouts  2.87 us (3%)
  other arithmetic  2.57 us (3%)
    all_to_all x1, blocking collectives, per_device(): plane = jnp.sum(lax.all_to_all(pair, YX, 0, 0, tiled=True), axis=0)  17.3 us
    all_to_all x1, blocking collectives, per_device(): summed = jnp.sum(lax.all_to_all(line, 'rows_2', 0, 0, tiled=True), axis=0)  15.6 us
    pallas_call x1, Pallas kernels, finish(): pl.pallas_call(finish_kernel, grid_spec=pltpu.PrefetchScalarGridSpec(num_...  12.3 us
    pallas_call x1, Pallas kernels, local_products(): pl.pallas_call(local_kernel, grid_spec=pltpu.PrefetchScalarGridSpec(num_s...  11.7 us
    ppermute x3, starting transfers between devices, swap_cores(): return lax.ppermute(x, 'rows_3', [(0, 1), (1, 0)])  7.32 us
    all_to_all x1, waiting for transfers between devices, per_device(): gmine = lax.all_to_all(copies, YX, 0, 0, tiled=True)  6.79 us
    all_to_all x1, starting transfers between devices, per_device(): gmine = lax.all_to_all(copies, YX, 0, 0, tiled=True)  3.51 us
    ppermute x3, waiting for transfers between devices, swap_cores(): return lax.ppermute(x, 'rows_3', [(0, 1), (1, 0)])  3.03 us
  transfers between devices with their start and end apart: 4, of which 3 were waited for; matrix products, arithmetic and copies ran while one was open for 0% of the time, Pallas kernels for 0%

commit v1 on v0

--- a/solution.py
+++ b/solution.py
@@ -23,6 +23,10 @@
     return lax.broadcasted_iota(jnp.int32, shape, dim)
 
 
+def in_hbm(x):
+    return pltpu.with_memory_space_constraint(x, pltpu.HBM)
+
+
 def matmul(a, b, dims=((1,), (0,)), precision=None):
     return lax.dot_general(
         a, b, (dims, ((), ())), preferred_element_type=jnp.float32, precision=precision
@@ -44,7 +48,7 @@
         sq8[...] = jnp.zeros_like(sq8)
         cross8[...] = jnp.zeros_like(cross8)
         pay[:, :, NZ:, :, :] = jnp.zeros((2, NYX, 2, 8, LANES), jnp.float32)
-        column = jnp.broadcast_to(block_row[...], (LANES, NCAND)).T
+        column = jnp.broadcast_to(block_row[...].astype(jnp.float32), (LANES, NCAND)).T
         for b in range(NB):
             masks[b] = jnp.where(column == float(b), 1.0, 0.0).astype(jnp.bfloat16)
 
@@ -98,7 +102,7 @@
                     :, LANES * h : LANES * (h + 1)
                 ]
         sq = jnp.sum(sq8[...], axis=0, keepdims=True)
-        same = block_row[...] == blocks[first].astype(jnp.float32)
+        same = block_row[...] == blocks[first]
         cross = jnp.where(same, cross8[0:1, :], 0.0)
         for q in range(NCAND // LANES):
             part = slice(LANES * q, LANES * (q + 1))
@@ -125,7 +129,6 @@
     fstep, wstep = rows // STEPS, wrows // STEPS
     groups = wrows // LANES
     payload = jax.ShapeDtypeStruct((NYX, SLOTS, 8, LANES), jnp.float32)
-    fixed4 = pl.BlockSpec((NYX, SLOTS, 8, LANES), lambda i, *_: (0, 0, 0, 0))
     return pl.pallas_call(
         local_kernel,
         grid_spec=pltpu.PrefetchScalarGridSpec(
@@ -136,11 +139,7 @@
                 pl.BlockSpec((wstep, NCAND), lambda i, *_: (i, 0)),
                 pl.BlockSpec((1, NCAND), lambda i, *_: (0, 0)),
             ],
-            out_specs=[
-                fixed4,
-                fixed4,
-                pl.BlockSpec((groups, 8, LANES * NB), lambda i, *_: (0, 0, 0)),
-            ],
+            out_specs=[pl.BlockSpec(memory_space=pltpu.VMEM)] * 3,
             scratch_shapes=[
                 pltpu.VMEM((2, fstep, LANES), jnp.float32),
                 pltpu.VMEM((NCAND, rank), jnp.float32),
@@ -154,16 +153,16 @@
         ),
         out_shape=[payload, payload, jax.ShapeDtypeStruct((groups, 8, LANES * NB), jnp.float32)],
         compiler_params=pltpu.CompilerParams(
-            dimension_semantics=("arbitrary",), vmem_limit_bytes=60 * 2**20
+            dimension_semantics=("arbitrary",), vmem_limit_bytes=44 * 2**20
         ),
         name="local",
     )(
         chosen,
         cand_block,
         core,
-        factor,
-        cand_weights,
-        cand_block.astype(jnp.float32).reshape(1, NCAND),
+        in_hbm(factor),
+        in_hbm(cand_weights),
+        cand_block.reshape(1, NCAND),
     )
 
 
@@ -306,9 +305,9 @@
             jax.ShapeDtypeStruct((2, 4), jnp.float32),
             jax.ShapeDtypeStruct((2, local_rows), jnp.float32),
         ],
-        compiler_params=pltpu.CompilerParams(vmem_limit_bytes=40 * 2**20),
+        compiler_params=pltpu.CompilerParams(vmem_limit_bytes=16 * 2**20),
         name="finish",
-    )(chosen, where, gmine, gtheirs, pmine, ptheirs, noise, dense, factor)
+    )(chosen, where, gmine, gtheirs, pmine, ptheirs, noise, dense, in_hbm(factor))
 
 
 def swap_cores(x):

time: 84.1 us -> 79 us (0.939)
  other arithmetic: 2.57 us -> 0.2 us
  Pallas kernels: 24 us -> 22.4 us
    pallas_call x1, Pallas kernels: 11.7 us -> 10.4 us  [local_products(): pl.pallas_call(local_kernel, grid_spec=pltpu.PrefetchScalarGridSpec(num_s...]
    convert_element_type x1 -> x0, other arithmetic: 1.28 us -> none  [local_products(): cand_block.astype(jnp.float32).reshape(1, NCAND)]
    add x1, other arithmetic: 1.16 us -> 0.07 us  [per_device(): pair = mine + swap_cores(theirs)]
    unnamed x8, local copies, waits for them, and re-layouts: 2.19 us -> 1.35 us
where the time goes in v1:
time: 79 us; the launch traced here: 78.7 us
  blocking collectives  32.8 us (42%)
  Pallas kernels  22.4 us (28%)
  starting transfers between devices  10.8 us (14%)
  waiting for transfers between devices  9.61 us (12%)
  local copies, waits for them, and re-layouts  2.03 us (3%)
    all_to_all x1, blocking collectives, per_device(): plane = jnp.sum(lax.all_to_all(pair, YX, 0, 0, tiled=True), axis=0)  17.3 us
    all_to_all x1, blocking collectives, per_device(): summed = jnp.sum(lax.all_to_all(line, 'rows_2', 0, 0, tiled=True), axis=0)  15.6 us
    pallas_call x1, Pallas kernels, finish(): pl.pallas_call(finish_kernel, grid_spec=pltpu.PrefetchScalarGridSpec(num_...  12.1 us
    pallas_call x1, Pallas kernels, local_products(): pl.pallas_call(local_kernel, grid_spec=pltpu.PrefetchScalarGridSpec(num_s...  10.4 us
    ppermute x3, starting transfers between devices, swap_cores(): return lax.ppermute(x, 'rows_3', [(0, 1), (1, 0)])  7.29 us
    all_to_all x1, waiting for transfers between devices, per_device(): gmine = lax.all_to_all(copies, YX, 0, 0, tiled=True)  6.79 us
    all_to_all x1, starting transfers between devices, per_device(): gmine = lax.all_to_all(copies, YX, 0, 0, tiled=True)  3.51 us
    ppermute x3, waiting for transfers between devices, swap_cores(): return lax.ppermute(x, 'rows_3', [(0, 1), (1, 0)])  2.81 us
  transfers between devices with their start and end apart: 4, of which 3 were waited for; matrix products, arithmetic and copies ran while one was open for 0% of the time, Pallas kernels for 0%

profile of v1, /device:TPU:1, one launch (start us, length us, event | category | flops | bytes accessed | tf_op | source)
XLA Modules:
  0.0 78.7 jit_solution(12419851561181268269)
XLA Ops:
  0.6 0.0 copy-start
  0.6 0.7 copy-done
  1.3 0.0 copy-start.2
  1.3 0.7 copy-done.2
  2.0 10.4 %local.1 = (f32[16,10,8,128]{3,2,1,0:T(8,128)S(1)}, f32[16,10,8,128]{3,2,1,0:T(8,128)S(1)}, f32[16,8,512]{2,1,0:T(8,128)S(1)}) custom-call(s32[2]{0:T(128)S(1)} %copy-done.2, s32[1024]{0:T(1024)S(1)} %copy-done, s32[1]{0:T(128)} %bitcast.core, bf16[8192,256]{1,0:T(8,128)(2,1)} %factor.1, bf16[2048,1024]{1,0:T(8,128)(2,1)} %wts.1, s32[1,1024]{1,0:T(1,128)S(1)} %bitcast.8), custom_call_target="tpu_custom_call" | custom-call | tf_op jit(solution)/shard_map/local/pallas_call | solution.py:132
  12.4 0.0 copy-start.1
  12.4 0.0 copy-start.3
  12.4 3.3 %collective-permute-start = (f32[16,10,8,128]{3,2,1,0:T(8,128)S(1)}, f32[16,10,8,128]{3,2,1,0:T(8,128)S(1)}, u32[]{:S(2)}, u32[]{:S(2)}) collective-permute-start(f32[16,10,8,128]{3,2,1,0:T(8,128)S(1)} %get-tuple-element.6), channel_id=1, source_target_pairs={{0,1},{1,0},{2,3},{3,2},{4,5},{5,4},{6,7},{7,6},{8,9},{9,8},{10,11... | collective-permute-start | bytes 1966088 | tf_op jit(solution)/shard_map/ppermute | solution.py:314
  15.6 1.7 %collective-permute-done = f32[16,10,8,128]{3,2,1,0:T(8,128)S(1)} collective-permute-done((f32[16,10,8,128]{3,2,1,0:T(8,128)S(1)}, f32[16,10,8,128]{3,2,1,0:T(8,128)S(1)}, u32[]{:S(2)}, u32[]{:S(2)}) %collective-permute-start) | collective-permute-done | bytes 655392 | tf_op jit(solution)/shard_map/ppermute | solution.py:314
  17.4 0.1 add.11
  17.4 17.3 %all_to_all.15 = f32[16,10,8,128]{3,2,1,0:T(8,128)S(1)} all-to-all(f32[16,10,8,128]{3,2,1,0:T(8,128)S(1)} %add.11), channel_id=1, replica_groups=mesh['rows_0'=4,'rows_1'=4,'rows_2'=8,'rows_3'=2] {'rows_0','rows_1'}, dimensions={0} | all-to-all | bytes 1310720 | tf_op jit(solution)/shard_map/all_to_all | solution.py:324
  34.8 15.6 %all_to_all.16 = f32[8,3,8,128]{3,2,1,0:T(8,128)S(1)} all-to-all(f32[8,3,8,128]{3,2,1,0:T(8,128)S(1)} %pad_maximum_fusion), channel_id=1, replica_groups=mesh['rows_0'=4,'rows_1'=4,'rows_2'=8,'rows_3'=2] {'rows_2'}, dimensions={0} | all-to-all | bytes 196608 | tf_op jit(solution)/shard_map/all_to_all | solution.py:327
  50.4 0.7 broadcast_in_dim.8
  51.1 3.5 %all-to-all-start.2 = ((f32[16,2,8,128]{3,2,1,0:T(8,128)}), f32[16,2,8,128]{3,2,1,0:T(8,128)S(1)}, u32[]{:S(2)}, u32[]{:S(2)}) async-start(f32[16,2,8,128]{3,2,1,0:T(8,128)} %broadcast_in_dim.8), calls=%async_computation.2 | async-start | bytes 262144 | tf_op jit(solution)/shard_map/all_to_all | solution.py:331
  54.6 6.8 %all-to-all-done.2.gmine = f32[16,2,8,128]{3,2,1,0:T(8,128)S(1)} async-done(((f32[16,2,8,128]{3,2,1,0:T(8,128)}), f32[16,2,8,128]{3,2,1,0:T(8,128)S(1)}, u32[]{:S(2)}, u32[]{:S(2)}) %all-to-all-start.2) | async-done | bytes 131104 | tf_op jit(solution)/shard_map/all_to_all | solution.py:331
  61.4 4.0 %collective-permute-start.1 = (f32[16,2,8,128]{3,2,1,0:T(8,128)S(1)}, f32[16,2,8,128]{3,2,1,0:T(8,128)S(1)}, u32[]{:S(2)}, u32[]{:S(2)}) collective-permute-start(f32[16,2,8,128]{3,2,1,0:T(8,128)S(1)} %all-to-all-done.2.gmine), channel_id=1, source_target_pairs={{0,1},{1,0},{2,3},{3,2},{4,5},{5,4},{6,7},{7,6},{8,9},{9,8},{10,11... | collective-permute-start | bytes 393224 | tf_op jit(solution)/shard_map/ppermute | solution.py:314
  65.4 0.0 collective-permute-start.2
  65.4 0.1 pad_add_fusion.where
  65.5 1.1 %collective-permute-done.2.ptheirs = f32[8,128]{1,0:T(8,128)S(1)} collective-permute-done((f32[8,128]{1,0:T(8,128)S(1)}, f32[8,128]{1,0:T(8,128)S(1)}, u32[]{:S(2)}, u32[]{:S(2)}) %collective-permute-start.2) | collective-permute-done | bytes 4128 | tf_op jit(solution)/shard_map/ppermute | solution.py:314
  66.6 0.0 collective-permute-done.1.gtheirs
  66.6 0.0 copy-done.1
  66.6 0.0 copy-done.3
  66.6 12.1 %finish.1 = (f32[2,4]{1,0:T(2,128)}, f32[2,8192]{1,0:T(2,128)}) custom-call(s32[2]{0:T(128)S(1)} %copy-done.3, s32[2]{0:T(128)S(1)} %pad_add_fusion.where, f32[16,2,8,128]{3,2,1,0:T(8,128)S(1)} %all-to-all-done.2.gmine, f32[16,2,8,128]{3,2,1,0:T(8,128)S(1)} %collective-permute-done.1.gtheirs, f32[8,128]{1,0:T(8,128)S(1)} %slice_bitcast_fusion.1.pmine, ...), custom_call_target="tpu_custom_call" | custom-call | tf_op jit(solution)/shard_map/finish/pallas_call | solution.py:290
  (8 shorter events, 0.1 us)
Async XLA Ops:
  0.6 0.7 copy-start
  1.3 0.7 copy-start.2
  12.4 54.2 %copy-start.1 = (f32[1024]{0:T(1024)S(1)}, f32[1024]{0:T(1024)}, u32[]{:S(2)}) copy-start(f32[1024]{0:T(1024)} %param.8) | copy-start | bytes 12292
  12.4 54.2 %copy-start.3 = (s32[2]{0:T(128)S(1)}, s32[2]{0:T(128)}, u32[]{:S(2)}) copy-start(s32[2]{0:T(128)} %chosen.3) | copy-start | bytes 28
  12.4 5.0 %collective-permute-start = (f32[16,10,8,128]{3,2,1,0:T(8,128)S(1)}, f32[16,10,8,128]{3,2,1,0:T(8,128)S(1)}, u32[]{:S(2)}, u32[]{:S(2)}) collective-permute-start(f32[16,10,8,128]{3,2,1,0:T(8,128)S(1)} %get-tuple-element.6), channel_id=1, source_target_pairs={{0,1},{1,0},{2,3},{3,2},{4,5},{5,4},{6,7},{7,6},{8,9},{9,8},{10,11... | collective-permute-start | bytes 1966088 | tf_op jit(solution)/shard_map/ppermute | solution.py:314
  51.1 10.3 %all-to-all-start.2 = ((f32[16,2,8,128]{3,2,1,0:T(8,128)}), f32[16,2,8,128]{3,2,1,0:T(8,128)S(1)}, u32[]{:S(2)}, u32[]{:S(2)}) async-start(f32[16,2,8,128]{3,2,1,0:T(8,128)} %broadcast_in_dim.8), calls=%async_computation.2 | async-start | bytes 262144 | tf_op jit(solution)/shard_map/all_to_all | solution.py:331
  61.4 5.2 %collective-permute-start.1 = (f32[16,2,8,128]{3,2,1,0:T(8,128)S(1)}, f32[16,2,8,128]{3,2,1,0:T(8,128)S(1)}, u32[]{:S(2)}, u32[]{:S(2)}) collective-permute-start(f32[16,2,8,128]{3,2,1,0:T(8,128)S(1)} %all-to-all-done.2.gmine), channel_id=1, source_target_pairs={{0,1},{1,0},{2,3},{3,2},{4,5},{5,4},{6,7},{7,6},{8,9},{9,8},{10,11... | collective-permute-start | bytes 393224 | tf_op jit(solution)/shard_map/ppermute | solution.py:314
  65.4 1.2 %collective-permute-start.2 = (f32[8,128]{1,0:T(8,128)S(1)}, f32[8,128]{1,0:T(8,128)S(1)}, u32[]{:S(2)}, u32[]{:S(2)}) collective-permute-start(f32[8,128]{1,0:T(8,128)S(1)} %slice_bitcast_fusion.1.pmine), channel_id=1, source_target_pairs={{0,1},{1,0},{2,3},{3,2},{4,5},{5,4},{6,7},{7,6},{8,9},{9,8},{10,11... | collective-permute-start | bytes 12296 | tf_op jit(solution)/shard_map/ppermute | solution.py:314

commit v2 on v1

--- a/solution.py
+++ b/solution.py
@@ -14,6 +14,7 @@
 NZ = 8
 SLOTS = NZ + 2
 STEPS = 4
+MILD = 1024.0
 ROWS = ("rows_0", "rows_1", "rows_2", "rows_3")
 YX = ("rows_0", "rows_1")
 HIGHEST = lax.Precision.HIGHEST
@@ -157,8 +158,8 @@
         ),
         name="local",
     )(
-        chosen,
-        cand_block,
+        in_hbm(chosen),
+        in_hbm(cand_block),
         core,
         in_hbm(factor),
         in_hbm(cand_weights),
@@ -166,6 +167,19 @@
     )
 
 
+def parts(x):
+    high = x.astype(jnp.bfloat16)
+    return high, (x - high.astype(jnp.float32)).astype(jnp.bfloat16)
+
+
+def paired(p, q):
+    ph, pl_ = parts(p)
+    qh, ql = parts(q)
+    return matmul(
+        jnp.concatenate([ph, pl_, ph], axis=1), jnp.concatenate([qh, qh, ql], axis=0)
+    )
+
+
 def total(x):
     return jnp.sum(jnp.sum(x, axis=1, keepdims=True), axis=0, keepdims=True)
 
@@ -175,7 +189,7 @@
 
 
 def finish_kernel(
-    chosen, where, gmine, gtheirs, pmine, ptheirs, noise, dense, factor, scores, updates,
+    chosen, where, mine, theirs, noise, dense, factor, scores, updates,
     fvmem, m, x, sem,
 ):
     copy = pltpu.make_async_copy(factor, fvmem, sem)
@@ -183,9 +197,11 @@
     core, chip = where[0], where[1]
     first, second = chosen[0], chosen[1]
     own = core == 0
-    a_, b_ = gmine[...], gtheirs[...]
-    g0 = jnp.where(own, a_, b_)
-    g1 = jnp.where(own, b_, a_)
+    a_, b_ = mine[...], theirs[...]
+    first_half = jnp.where(own, a_, b_)
+    second_half = jnp.where(own, b_, a_)
+    g0 = first_half[: 2 * NYX].reshape(NYX, 2, 8, LANES)
+    g1 = second_half[: 2 * NYX].reshape(NYX, 2, 8, LANES)
     half = NYX // 2
     top = g0[:, 0].reshape(LANES, LANES)
     side = g1[:, 0].reshape(LANES, LANES)
@@ -196,8 +212,7 @@
     m[LANES:, :LANES] = side.T
     m[LANES:, LANES:] = low + jnp.where(diag, 1.0, 0.0)
     psel, sq, cross = g0[half, 1], g1[half, 1], g1[half + 1, 1]
-    p_, q_ = pmine[...], ptheirs[...]
-    pown = jnp.concatenate([jnp.where(own, p_, q_), jnp.where(own, q_, p_)], axis=1)
+    pown = jnp.concatenate([first_half[2 * NYX], second_half[2 * NYX]], axis=1)
     pj = jnp.concatenate([psel[0:1], psel[1:2]], axis=1)
     pk = jnp.concatenate([psel[2:3], psel[3:4]], axis=1)
     rid = iota((8, R), 0)
@@ -214,20 +229,33 @@
     x[...] = (scale0 * alpha) * (2.0 * eye - alpha * full)
     rho1 = rho0 * rho0 / (2.0 - rho0 * rho0)
 
-    def newton(carry):
-        rho, count = carry
-        scale = 2.0 / (2.0 - rho * rho)
-        now = x[...]
-        prod = matmul(m[...], now, precision=HIGHEST)
-        x[...] = scale * (2.0 * now - matmul(now, prod, precision=HIGHEST))
-        return rho * rho / (2.0 - rho * rho), count + 1
-
-    lax.while_loop(lambda s: (s[0] > 5e-3) & (s[1] < 100), newton, (rho1, jnp.int32(0)))
-    inv = x[...]
-    a = matmul(rhs, inv, precision=HIGHEST)
-    for _ in range(2):
-        left = rhs - matmul(a, full, precision=HIGHEST)
-        a = a + matmul(left, inv, precision=HIGHEST)
+    def precise(p, q):
+        return matmul(p, q, precision=HIGHEST)
+
+    def newton(product):
+        def body(carry):
+            rho, count = carry
+            scale = 2.0 / (2.0 - rho * rho)
+            now = x[...]
+            x[...] = scale * (2.0 * now - product(now, product(m[...], now)))
+            return rho * rho / (2.0 - rho * rho), count + 1
+
+        return body
+
+    mild = bound < MILD
+    state = lax.while_loop(
+        lambda s: mild & (s[0] > 5e-3) & (s[1] < 100), newton(paired), (rho1, jnp.int32(0))
+    )
+    lax.while_loop(lambda s: (s[0] > 5e-3) & (s[1] < 100), newton(precise), state)
+
+    def solved(product):
+        inv, system = x[...], m[...]
+        a = product(rhs, inv)
+        for _ in range(2):
+            a = a + product(rhs - precise(a, system), inv)
+        return a
+
+    a = lax.cond(mild, lambda: solved(paired), lambda: solved(precise))
 
     aown, aboth = a[:8], a[8:]
     aj, ak = aboth[0:1], aboth[1:2]
@@ -284,7 +312,7 @@
         updates[1:2, part] = (left[1:2] - w1 * ratio) * r2
 
 
-def finish(gmine, gtheirs, pmine, ptheirs, noise, dense, factor, chosen, where):
+def finish(mine, theirs, noise, dense, factor, chosen, where):
     local_rows = factor.shape[0]
     vmem = pl.BlockSpec(memory_space=pltpu.VMEM)
     return pl.pallas_call(
@@ -292,7 +320,7 @@
         grid_spec=pltpu.PrefetchScalarGridSpec(
             num_scalar_prefetch=2,
             grid=(),
-            in_specs=[vmem] * 6 + [pl.BlockSpec(memory_space=pl.ANY)],
+            in_specs=[vmem] * 4 + [pl.BlockSpec(memory_space=pl.ANY)],
             out_specs=[vmem, vmem],
             scratch_shapes=[
                 pltpu.VMEM(factor.shape, jnp.bfloat16),
@@ -307,7 +335,7 @@
         ],
         compiler_params=pltpu.CompilerParams(vmem_limit_bytes=16 * 2**20),
         name="finish",
-    )(chosen, where, gmine, gtheirs, pmine, ptheirs, noise, dense, in_hbm(factor))
+    )(in_hbm(chosen), where, mine, theirs, noise, dense, in_hbm(factor))
 
 
 def swap_cores(x):
@@ -317,22 +345,19 @@
 def per_device(factor, cand_weights, cand_block, noise, chosen):
     core = lax.axis_index("rows_3").astype(jnp.int32)
     chip = lax.axis_index(("rows_0", "rows_1", "rows_2")).astype(jnp.int32)
-    mine, theirs, dense = local_products(
-        factor, cand_weights, cand_block, chosen, core.reshape(1)
-    )
+    where = jnp.stack([core, chip])
+    mine, theirs, dense = local_products(factor, cand_weights, cand_block, chosen, where)
     pair = mine + swap_cores(theirs)
     plane = jnp.sum(lax.all_to_all(pair, YX, 0, 0, tiled=True), axis=0)
     shared = jnp.broadcast_to(plane[None, NZ:], (NZ, 2, 8, LANES))
     line = jnp.concatenate([plane[:NZ, None], shared], axis=1)
     summed = jnp.sum(lax.all_to_all(line, "rows_2", 0, 0, tiled=True), axis=0)
-    pmine = summed[0]
-    ptheirs = swap_cores(pmine)
-    copies = jnp.broadcast_to(summed[None, 1:], (NYX, 2, 8, LANES))
-    gmine = lax.all_to_all(copies, YX, 0, 0, tiled=True)
-    gtheirs = swap_cores(gmine)
+    shared = jnp.broadcast_to(summed[None, 1:], (NYX, 2, 8, LANES))
+    shared, own = lax.optimization_barrier((shared, summed[:1]))
+    gathered = lax.all_to_all(shared, YX, 0, 0, tiled=True)
+    known = jnp.concatenate([gathered.reshape(2 * NYX, 8, LANES), own], axis=0)
     scores, updates = finish(
-        gmine, gtheirs, pmine, ptheirs, noise.reshape(8, LANES), dense, factor, chosen,
-        jnp.stack([core, chip]),
+        known, swap_cores(known), noise.reshape(8, LANES), dense, factor, chosen, where
     )
     return scores, updates
 

time: 79 us -> 76.6 us (0.970)
  blocking collectives: 32.8 us -> 42.9 us
  waiting for transfers between devices: 9.61 us -> 2.72 us
  starting transfers between devices: 10.8 us -> 7.32 us
  local copies, waits for them, and re-layouts: 2.03 us -> 0.04 us
    all_to_all x0 -> x1, blocking collectives: none -> 10 us  [per_device(): gathered = lax.all_to_all(shared, YX, 0, 0, tiled=True)]
    all_to_all x1 -> x0, waiting for transfers between devices: 6.79 us -> none  [per_device(): gmine = lax.all_to_all(copies, YX, 0, 0, tiled=True)]
    all_to_all x1 -> x0, starting transfers between devices: 3.51 us -> none  [per_device(): gmine = lax.all_to_all(copies, YX, 0, 0, tiled=True)]
    unnamed x8 -> x2, local copies, waits for them, and re-layouts: 1.35 us -> 0.01 us
    ppermute x3 -> x2, waiting for transfers between devices: 2.81 us -> 2.72 us  [swap_cores(): return lax.ppermute(x, 'rows_3', [(0, 1), (1, 0)])]
    ppermute x3 -> x2, starting transfers between devices: 7.29 us -> 7.32 us  [swap_cores(): return lax.ppermute(x, 'rows_3', [(0, 1), (1, 0)])]
  transfers between devices with their start and end apart: 4 -> 2, of which waited for: 3 -> 2; matrix products, arithmetic and copies ran while one was open for 0% -> 0% of each run, Pallas kernels for 0% -> 0%
where the time goes in v2:
time: 76.6 us; the launch traced here: 76.4 us
  blocking collectives  42.9 us (56%)
  Pallas kernels  22.5 us (29%)
  starting transfers between devices  7.32 us (10%)
  waiting for transfers between devices  2.72 us (4%)
    all_to_all x1, blocking collectives, per_device(): plane = jnp.sum(lax.all_to_all(pair, YX, 0, 0, tiled=True), axis=0)  17.3 us
    all_to_all x1, blocking collectives, per_device(): summed = jnp.sum(lax.all_to_all(line, 'rows_2', 0, 0, tiled=True), axis=0)  15.6 us
    pallas_call x1, Pallas kernels, finish(): pl.pallas_call(finish_kernel, grid_spec=pltpu.PrefetchScalarGridSpec(num_...  12 us
    pallas_call x1, Pallas kernels, local_products(): pl.pallas_call(local_kernel, grid_spec=pltpu.PrefetchScalarGridSpec(num_s...  10.5 us
    all_to_all x1, blocking collectives, per_device(): gathered = lax.all_to_all(shared, YX, 0, 0, tiled=True)  10 us
    ppermute x2, starting transfers between devices, swap_cores(): return lax.ppermute(x, 'rows_3', [(0, 1), (1, 0)])  7.32 us
    ppermute x2, waiting for transfers between devices, swap_cores(): return lax.ppermute(x, 'rows_3', [(0, 1), (1, 0)])  2.72 us
  transfers between devices with their start and end apart: 2, of which 2 were waited for; matrix products, arithmetic and copies ran while one was open for 0% of the time, Pallas kernels for 0%

profile of v2, /device:TPU:1, one launch (start us, length us, event | category | flops | bytes accessed | tf_op | source)
XLA Modules:
  0.0 76.4 jit_solution(14339215198695555408)
XLA Ops:
  0.6 0.1 pad_add_fusion.core.where
  0.7 10.5 %local.1 = (f32[16,10,8,128]{3,2,1,0:T(8,128)S(1)}, f32[16,10,8,128]{3,2,1,0:T(8,128)S(1)}, f32[16,8,512]{2,1,0:T(8,128)S(1)}) custom-call(s32[2]{0:T(128)} %chosen.3, s32[1024]{0:T(1024)} %blocks.1, s32[2]{0:T(128)S(1)} %pad_add_fusion.core.where, bf16[8192,256]{1,0:T(8,128)(2,1)} %factor.1, bf16[2048,1024]{1,0:T(8,128)(2,1)} %wts.1, s32[1,1024]{1,0:T(1,128)} %bitcast.9), custom_call_target="tpu_custom_call" | custom-call | tf_op jit(solution)/shard_map/local/pallas_call | solution.py:133
  11.2 0.0 copy-start
  11.2 3.3 %collective-permute-start = (f32[16,10,8,128]{3,2,1,0:T(8,128)S(1)}, f32[16,10,8,128]{3,2,1,0:T(8,128)S(1)}, u32[]{:S(2)}, u32[]{:S(2)}) collective-permute-start(f32[16,10,8,128]{3,2,1,0:T(8,128)S(1)} %get-tuple-element.8), channel_id=1, source_target_pairs={{0,1},{1,0},{2,3},{3,2},{4,5},{5,4},{6,7},{7,6},{8,9},{9,8},{10,11... | collective-permute-start | bytes 1966088 | tf_op jit(solution)/shard_map/ppermute | solution.py:342
  14.5 1.7 %collective-permute-done = f32[16,10,8,128]{3,2,1,0:T(8,128)S(1)} collective-permute-done((f32[16,10,8,128]{3,2,1,0:T(8,128)S(1)}, f32[16,10,8,128]{3,2,1,0:T(8,128)S(1)}, u32[]{:S(2)}, u32[]{:S(2)}) %collective-permute-start) | collective-permute-done | bytes 655392 | tf_op jit(solution)/shard_map/ppermute | solution.py:342
  16.3 0.1 add.11
  16.3 17.3 %all_to_all.15 = f32[16,10,8,128]{3,2,1,0:T(8,128)S(1)} all-to-all(f32[16,10,8,128]{3,2,1,0:T(8,128)S(1)} %add.11), channel_id=1, replica_groups=mesh['rows_0'=4,'rows_1'=4,'rows_2'=8,'rows_3'=2] {'rows_0','rows_1'}, dimensions={0} | all-to-all | bytes 1310720 | tf_op jit(solution)/shard_map/all_to_all | solution.py:351
  33.7 15.6 %all_to_all.16 = f32[8,3,8,128]{3,2,1,0:T(8,128)S(1)} all-to-all(f32[8,3,8,128]{3,2,1,0:T(8,128)S(1)} %pad_maximum_fusion.1), channel_id=1, replica_groups=mesh['rows_0'=4,'rows_1'=4,'rows_2'=8,'rows_3'=2] {'rows_2'}, dimensions={0} | all-to-all | bytes 196608 | tf_op jit(solution)/shard_map/all_to_all | solution.py:354
  49.3 10.0 %all_to_all.17 = f32[16,2,8,128]{3,2,1,0:T(8,128)S(1)} all-to-all(f32[16,2,8,128]{3,2,1,0:T(8,128)S(1)} %broadcast_in_dim.8), channel_id=1, replica_groups=mesh['rows_0'=4,'rows_1'=4,'rows_2'=8,'rows_3'=2] {'rows_0','rows_1'}, dimensions={0} | all-to-all | bytes 262144 | tf_op jit(solution)/shard_map/all_to_all | solution.py:357
  59.3 4.0 %collective-permute-start.1 = (f32[33,8,128]{2,1,0:T(8,128)S(1)}, f32[33,8,128]{2,1,0:T(8,128)S(1)}, u32[]{:S(2)}, u32[]{:S(2)}) collective-permute-start(f32[33,8,128]{2,1,0:T(8,128)S(1)} %pad_maximum_fusion.mine), channel_id=1, source_target_pairs={{0,1},{1,0},{2,3},{3,2},{4,5},{5,4},{6,7},{7,6},{8,9},{9,8},{10,11... | collective-permute-start | bytes 405512 | tf_op jit(solution)/shard_map/ppermute | solution.py:342
  63.4 1.0 %collective-permute-done.1.theirs = f32[33,8,128]{2,1,0:T(8,128)S(1)} collective-permute-done((f32[33,8,128]{2,1,0:T(8,128)S(1)}, f32[33,8,128]{2,1,0:T(8,128)S(1)}, u32[]{:S(2)}, u32[]{:S(2)}) %collective-permute-start.1) | collective-permute-done | bytes 135200 | tf_op jit(solution)/shard_map/ppermute | solution.py:342
  64.4 0.0 copy-done
  64.4 12.0 %finish.1 = (f32[2,4]{1,0:T(2,128)}, f32[2,8192]{1,0:T(2,128)}) custom-call(s32[2]{0:T(128)} %chosen.3, s32[2]{0:T(128)S(1)} %pad_add_fusion.core.where, f32[33,8,128]{2,1,0:T(8,128)S(1)} %pad_maximum_fusion.mine, f32[33,8,128]{2,1,0:T(8,128)S(1)} %collective-permute-done.1.theirs, f32[8,128]{1,0:T(8,128)S(1)} %bitcast.7, ...), custom_call_target="tpu_custom_call" | custom-call | tf_op jit(solution)/shard_map/finish/pallas_call | solution.py:318
  (10 shorter events, 0.1 us)
Async XLA Ops:
  11.2 53.1 %copy-start = (f32[1024]{0:T(1024)S(1)}, f32[1024]{0:T(1024)}, u32[]{:S(2)}) copy-start(f32[1024]{0:T(1024)} %param.8) | copy-start | bytes 12292
  11.2 5.0 %collective-permute-start = (f32[16,10,8,128]{3,2,1,0:T(8,128)S(1)}, f32[16,10,8,128]{3,2,1,0:T(8,128)S(1)}, u32[]{:S(2)}, u32[]{:S(2)}) collective-permute-start(f32[16,10,8,128]{3,2,1,0:T(8,128)S(1)} %get-tuple-element.8), channel_id=1, source_target_pairs={{0,1},{1,0},{2,3},{3,2},{4,5},{5,4},{6,7},{7,6},{8,9},{9,8},{10,11... | collective-permute-start | bytes 1966088 | tf_op jit(solution)/shard_map/ppermute | solution.py:342
  59.3 5.0 %collective-permute-start.1 = (f32[33,8,128]{2,1,0:T(8,128)S(1)}, f32[33,8,128]{2,1,0:T(8,128)S(1)}, u32[]{:S(2)}, u32[]{:S(2)}) collective-permute-start(f32[33,8,128]{2,1,0:T(8,128)S(1)} %pad_maximum_fusion.mine), channel_id=1, source_target_pairs={{0,1},{1,0},{2,3},{3,2},{4,5},{5,4},{6,7},{7,6},{8,9},{9,8},{10,11... | collective-permute-start | bytes 405512 | tf_op jit(solution)/shard_map/ppermute | solution.py:342

commit v3 on v2

--- a/solution.py
+++ b/solution.py
@@ -15,6 +15,7 @@
 SLOTS = NZ + 2
 STEPS = 4
 MILD = 1024.0
+RHO = 1e-2
 ROWS = ("rows_0", "rows_1", "rows_2", "rows_3")
 YX = ("rows_0", "rows_1")
 HIGHEST = lax.Precision.HIGHEST
@@ -220,17 +221,32 @@
     rhs = jnp.concatenate([pown, pboth], axis=0)
 
     full = m[...]
-    rowmax = jnp.max(jnp.sum(jnp.abs(full), axis=0, keepdims=True))
-    bound = jnp.maximum(rowmax, 1.0)
+    reach = jnp.max(jnp.sum(jnp.abs(full), axis=0, keepdims=True))
+    mild = reach < MILD
+    unit = full * (1.0 / reach)
+
+    def precise(p, q):
+        return matmul(p, q, precision=HIGHEST)
+
+    @pl.when(mild)
+    def _():
+        x[...] = paired(unit, unit)
+
+    @pl.when(jnp.logical_not(mild))
+    def _():
+        x[...] = precise(unit, unit)
+
+    square = x[...]
+    norm = jnp.sqrt(jnp.max(total(square * square)))
+    bound = jnp.maximum(reach * jnp.minimum(1.001 * jnp.sqrt(norm), 1.0), 1.0)
     rho0 = (bound - 1.0) / (bound + 1.0)
     alpha = 2.0 / (bound + 1.0)
+    grow = alpha * (2.0 / (2.0 - rho0 * rho0))
+    rho1 = rho0 * rho0 / (2.0 - rho0 * rho0)
+    scale1 = 2.0 / (2.0 - rho1 * rho1)
     eye = jnp.where(iota((R, R), 0) == iota((R, R), 1), 1.0, 0.0)
-    scale0 = 2.0 / (2.0 - rho0 * rho0)
-    x[...] = (scale0 * alpha) * (2.0 * eye - alpha * full)
-    rho1 = rho0 * rho0 / (2.0 - rho0 * rho0)
-
-    def precise(p, q):
-        return matmul(p, q, precision=HIGHEST)
+    start = grow * (2.0 * eye - alpha * full)
+    prod1 = (grow * reach) * (2.0 * unit - (alpha * reach) * square)
 
     def newton(product):
         def body(carry):
@@ -242,11 +258,19 @@
 
         return body
 
-    mild = bound < MILD
+    @pl.when(mild)
+    def _():
+        x[...] = scale1 * (2.0 * start - paired(start, prod1))
+
+    @pl.when(jnp.logical_not(mild))
+    def _():
+        x[...] = scale1 * (2.0 * start - precise(start, prod1))
+
+    rho2 = rho1 * rho1 / (2.0 - rho1 * rho1)
     state = lax.while_loop(
-        lambda s: mild & (s[0] > 5e-3) & (s[1] < 100), newton(paired), (rho1, jnp.int32(0))
-    )
-    lax.while_loop(lambda s: (s[0] > 5e-3) & (s[1] < 100), newton(precise), state)
+        lambda s: mild & (s[0] > RHO) & (s[1] < 100), newton(paired), (rho2, jnp.int32(0))
+    )
+    lax.while_loop(lambda s: (s[0] > RHO) & (s[1] < 100), newton(precise), state)
 
     def solved(product):
         inv, system = x[...], m[...]
@@ -255,7 +279,31 @@
             a = a + product(rhs - precise(a, system), inv)
         return a
 
-    a = lax.cond(mild, lambda: solved(paired), lambda: solved(precise))
+    def thirds(v):
+        high = v.astype(jnp.bfloat16)
+        rest = v - high.astype(jnp.float32)
+        mid = rest.astype(jnp.bfloat16)
+        return high, mid, (rest - mid.astype(jnp.float32)).astype(jnp.bfloat16)
+
+    def quick():
+        ih, il = parts(x[...])
+
+        def apply(v):
+            stack = jnp.concatenate(parts(v), axis=0)
+            one = matmul(stack, ih)
+            return one[:16] + (one[16:] + matmul(stack[:16], il))
+
+        mh, mm, ml = thirds(m[...])
+        a = apply(rhs)
+        for _ in range(2):
+            stack = jnp.concatenate(thirds(a), axis=0)
+            one = matmul(stack, mh)
+            two = matmul(stack[:32], mm)
+            back = one[:16] + ((one[16:32] + two[:16]) + (one[32:] + two[16:] + matmul(stack[:16], ml)))
+            a = a + apply(rhs - back)
+        return a
+
+    a = lax.cond(mild, quick, lambda: solved(precise))
 
     aown, aboth = a[:8], a[8:]
     aj, ak = aboth[0:1], aboth[1:2]

time: 76.6 us -> 75.5 us (0.986)
  Pallas kernels: 22.5 us -> 21.4 us
    pallas_call x1, Pallas kernels: 12 us -> 10.9 us  [finish(): pl.pallas_call(finish_kernel, grid_spec=pltpu.PrefetchScalarGridSpec(num_...]
where the time goes in v3:
time: 75.5 us; the launch traced here: 75.3 us
  blocking collectives  42.9 us (57%)
  Pallas kernels  21.4 us (28%)
  starting transfers between devices  7.32 us (10%)
  waiting for transfers between devices  2.72 us (4%)
    all_to_all x1, blocking collectives, per_device(): plane = jnp.sum(lax.all_to_all(pair, YX, 0, 0, tiled=True), axis=0)  17.3 us
    all_to_all x1, blocking collectives, per_device(): summed = jnp.sum(lax.all_to_all(line, 'rows_2', 0, 0, tiled=True), axis=0)  15.6 us
    pallas_call x1, Pallas kernels, finish(): pl.pallas_call(finish_kernel, grid_spec=pltpu.PrefetchScalarGridSpec(num_...  10.9 us
    pallas_call x1, Pallas kernels, local_products(): pl.pallas_call(local_kernel, grid_spec=pltpu.PrefetchScalarGridSpec(num_s...  10.5 us
    all_to_all x1, blocking collectives, per_device(): gathered = lax.all_to_all(shared, YX, 0, 0, tiled=True)  10 us
    ppermute x2, starting transfers between devices, swap_cores(): return lax.ppermute(x, 'rows_3', [(0, 1), (1, 0)])  7.32 us
    ppermute x2, waiting for transfers between devices, swap_cores(): return lax.ppermute(x, 'rows_3', [(0, 1), (1, 0)])  2.72 us
  transfers between devices with their start and end apart: 2, of which 2 were waited for; matrix products, arithmetic and copies ran while one was open for 0% of the time, Pallas kernels for 0%

profile of v3, /device:TPU:1, one launch (start us, length us, event | category | flops | bytes accessed | tf_op | source)
XLA Modules:
  0.0 75.3 jit_solution(15993190045246989644)
XLA Ops:
  0.6 0.1 pad_add_fusion.core.where
  0.7 10.5 %local.1 = (f32[16,10,8,128]{3,2,1,0:T(8,128)S(1)}, f32[16,10,8,128]{3,2,1,0:T(8,128)S(1)}, f32[16,8,512]{2,1,0:T(8,128)S(1)}) custom-call(s32[2]{0:T(128)} %chosen.3, s32[1024]{0:T(1024)} %blocks.1, s32[2]{0:T(128)S(1)} %pad_add_fusion.core.where, bf16[8192,256]{1,0:T(8,128)(2,1)} %factor.1, bf16[2048,1024]{1,0:T(8,128)(2,1)} %wts.1, s32[1,1024]{1,0:T(1,128)} %bitcast.9), custom_call_target="tpu_custom_call" | custom-call | tf_op jit(solution)/shard_map/local/pallas_call | solution.py:134
  11.2 0.0 copy-start
  11.2 3.3 %collective-permute-start = (f32[16,10,8,128]{3,2,1,0:T(8,128)S(1)}, f32[16,10,8,128]{3,2,1,0:T(8,128)S(1)}, u32[]{:S(2)}, u32[]{:S(2)}) collective-permute-start(f32[16,10,8,128]{3,2,1,0:T(8,128)S(1)} %get-tuple-element.8), channel_id=1, source_target_pairs={{0,1},{1,0},{2,3},{3,2},{4,5},{5,4},{6,7},{7,6},{8,9},{9,8},{10,11... | collective-permute-start | bytes 1966088 | tf_op jit(solution)/shard_map/ppermute | solution.py:390
  14.5 1.7 %collective-permute-done = f32[16,10,8,128]{3,2,1,0:T(8,128)S(1)} collective-permute-done((f32[16,10,8,128]{3,2,1,0:T(8,128)S(1)}, f32[16,10,8,128]{3,2,1,0:T(8,128)S(1)}, u32[]{:S(2)}, u32[]{:S(2)}) %collective-permute-start) | collective-permute-done | bytes 655392 | tf_op jit(solution)/shard_map/ppermute | solution.py:390
  16.2 0.1 add.11
  16.3 17.3 %all_to_all.15 = f32[16,10,8,128]{3,2,1,0:T(8,128)S(1)} all-to-all(f32[16,10,8,128]{3,2,1,0:T(8,128)S(1)} %add.11), channel_id=1, replica_groups=mesh['rows_0'=4,'rows_1'=4,'rows_2'=8,'rows_3'=2] {'rows_0','rows_1'}, dimensions={0} | all-to-all | bytes 1310720 | tf_op jit(solution)/shard_map/all_to_all | solution.py:399
  33.7 15.6 %all_to_all.16 = f32[8,3,8,128]{3,2,1,0:T(8,128)S(1)} all-to-all(f32[8,3,8,128]{3,2,1,0:T(8,128)S(1)} %pad_maximum_fusion.1), channel_id=1, replica_groups=mesh['rows_0'=4,'rows_1'=4,'rows_2'=8,'rows_3'=2] {'rows_2'}, dimensions={0} | all-to-all | bytes 196608 | tf_op jit(solution)/shard_map/all_to_all | solution.py:402
  49.3 10.0 %all_to_all.17 = f32[16,2,8,128]{3,2,1,0:T(8,128)S(1)} all-to-all(f32[16,2,8,128]{3,2,1,0:T(8,128)S(1)} %broadcast_in_dim.8), channel_id=1, replica_groups=mesh['rows_0'=4,'rows_1'=4,'rows_2'=8,'rows_3'=2] {'rows_0','rows_1'}, dimensions={0} | all-to-all | bytes 262144 | tf_op jit(solution)/shard_map/all_to_all | solution.py:405
  59.3 4.0 %collective-permute-start.1 = (f32[33,8,128]{2,1,0:T(8,128)S(1)}, f32[33,8,128]{2,1,0:T(8,128)S(1)}, u32[]{:S(2)}, u32[]{:S(2)}) collective-permute-start(f32[33,8,128]{2,1,0:T(8,128)S(1)} %pad_maximum_fusion.mine), channel_id=1, source_target_pairs={{0,1},{1,0},{2,3},{3,2},{4,5},{5,4},{6,7},{7,6},{8,9},{9,8},{10,11... | collective-permute-start | bytes 405512 | tf_op jit(solution)/shard_map/ppermute | solution.py:390
  63.3 1.0 %collective-permute-done.1.theirs = f32[33,8,128]{2,1,0:T(8,128)S(1)} collective-permute-done((f32[33,8,128]{2,1,0:T(8,128)S(1)}, f32[33,8,128]{2,1,0:T(8,128)S(1)}, u32[]{:S(2)}, u32[]{:S(2)}) %collective-permute-start.1) | collective-permute-done | bytes 135200 | tf_op jit(solution)/shard_map/ppermute | solution.py:390
  64.3 0.0 copy-done
  64.3 10.9 %finish.1 = (f32[2,4]{1,0:T(2,128)}, f32[2,8192]{1,0:T(2,128)}) custom-call(s32[2]{0:T(128)} %chosen.3, s32[2]{0:T(128)S(1)} %pad_add_fusion.core.where, f32[33,8,128]{2,1,0:T(8,128)S(1)} %pad_maximum_fusion.mine, f32[33,8,128]{2,1,0:T(8,128)S(1)} %collective-permute-done.1.theirs, f32[8,128]{1,0:T(8,128)S(1)} %bitcast.7, ...), custom_call_target="tpu_custom_call" | custom-call | tf_op jit(solution)/shard_map/finish/pallas_call | solution.py:366
  (10 shorter events, 0.1 us)
Async XLA Ops:
  11.2 53.1 %copy-start = (f32[1024]{0:T(1024)S(1)}, f32[1024]{0:T(1024)}, u32[]{:S(2)}) copy-start(f32[1024]{0:T(1024)} %param.8) | copy-start | bytes 12292
  11.2 5.0 %collective-permute-start = (f32[16,10,8,128]{3,2,1,0:T(8,128)S(1)}, f32[16,10,8,128]{3,2,1,0:T(8,128)S(1)}, u32[]{:S(2)}, u32[]{:S(2)}) collective-permute-start(f32[16,10,8,128]{3,2,1,0:T(8,128)S(1)} %get-tuple-element.8), channel_id=1, source_target_pairs={{0,1},{1,0},{2,3},{3,2},{4,5},{5,4},{6,7},{7,6},{8,9},{9,8},{10,11... | collective-permute-start | bytes 1966088 | tf_op jit(solution)/shard_map/ppermute | solution.py:390
  59.3 5.0 %collective-permute-start.1 = (f32[33,8,128]{2,1,0:T(8,128)S(1)}, f32[33,8,128]{2,1,0:T(8,128)S(1)}, u32[]{:S(2)}, u32[]{:S(2)}) collective-permute-start(f32[33,8,128]{2,1,0:T(8,128)S(1)} %pad_maximum_fusion.mine), channel_id=1, source_target_pairs={{0,1},{1,0},{2,3},{3,2},{4,5},{5,4},{6,7},{7,6},{8,9},{9,8},{10,11... | collective-permute-start | bytes 405512 | tf_op jit(solution)/shard_map/ppermute | solution.py:390

commit v4 on v3

--- a/solution.py
+++ b/solution.py
@@ -58,8 +58,9 @@
     for h in range(2):
         fwide[h] = fac[:, LANES * h : LANES * (h + 1)].astype(jnp.float32)
     turned = w.T
+    f = fac[...]
+    gram[...] += matmul(f.T, f)
     total = acc[...]
-    gsum = gram[...]
     for b in range(NB):
         fb = jnp.concatenate(
             [fwide[h, pl.ds(b, wrows, stride=NB), :] for h in range(2)], axis=1
@@ -69,9 +70,7 @@
             [turned[:, LANES * q : LANES * (q + 1)] * mask for q in range(wrows // LANES)], axis=1
         )
         total = total + matmul(seen, fb)
-        gsum = gsum + matmul(fb, fb, ((0,), (0,)))
     acc[...] = total
-    gram[...] = gsum
     wf = w.astype(jnp.float32)
     sq8[...] += jnp.sum((wf * wf).reshape(wrows // 8, 8, NCAND), axis=0)
     rows = iota((16, LANES), 0)

time: 75.5 us -> 75.3 us (level)
  no operation moved by 1% of the time
where the time goes in v4:
time: 75.3 us; the launch traced here: 75 us
  blocking collectives  42.9 us (57%)
  Pallas kernels  21.2 us (28%)
  starting transfers between devices  7.32 us (10%)
  waiting for transfers between devices  2.72 us (4%)
    all_to_all x1, blocking collectives, per_device(): plane = jnp.sum(lax.all_to_all(pair, YX, 0, 0, tiled=True), axis=0)  17.3 us
    all_to_all x1, blocking collectives, per_device(): summed = jnp.sum(lax.all_to_all(line, 'rows_2', 0, 0, tiled=True), axis=0)  15.6 us
    pallas_call x1, Pallas kernels, finish(): pl.pallas_call(finish_kernel, grid_spec=pltpu.PrefetchScalarGridSpec(num_...  10.9 us
    pallas_call x1, Pallas kernels, local_products(): pl.pallas_call(local_kernel, grid_spec=pltpu.PrefetchScalarGridSpec(num_s...  10.2 us
    all_to_all x1, blocking collectives, per_device(): gathered = lax.all_to_all(shared, YX, 0, 0, tiled=True)  10 us
    ppermute x2, starting transfers between devices, swap_cores(): return lax.ppermute(x, 'rows_3', [(0, 1), (1, 0)])  7.32 us
    ppermute x2, waiting for transfers between devices, swap_cores(): return lax.ppermute(x, 'rows_3', [(0, 1), (1, 0)])  2.72 us
  transfers between devices with their start and end apart: 2, of which 2 were waited for; matrix products, arithmetic and copies ran while one was open for 0% of the time, Pallas kernels for 0%

profile of v4, /device:TPU:1, one launch (start us, length us, event | category | flops | bytes accessed | tf_op | source)
XLA Modules:
  0.0 75.0 jit_solution(9449302610324631909)
XLA Ops:
  0.6 0.1 pad_add_fusion.core.where
  0.7 10.2 %local.1 = (f32[16,10,8,128]{3,2,1,0:T(8,128)S(1)}, f32[16,10,8,128]{3,2,1,0:T(8,128)S(1)}, f32[16,8,512]{2,1,0:T(8,128)S(1)}) custom-call(s32[2]{0:T(128)} %chosen.3, s32[1024]{0:T(1024)} %blocks.1, s32[2]{0:T(128)S(1)} %pad_add_fusion.core.where, bf16[8192,256]{1,0:T(8,128)(2,1)} %factor.1, bf16[2048,1024]{1,0:T(8,128)(2,1)} %wts.1, s32[1,1024]{1,0:T(1,128)} %bitcast.9), custom_call_target="tpu_custom_call" | custom-call | tf_op jit(solution)/shard_map/local/pallas_call | solution.py:133
  11.0 0.0 copy-start
  11.0 3.3 %collective-permute-start = (f32[16,10,8,128]{3,2,1,0:T(8,128)S(1)}, f32[16,10,8,128]{3,2,1,0:T(8,128)S(1)}, u32[]{:S(2)}, u32[]{:S(2)}) collective-permute-start(f32[16,10,8,128]{3,2,1,0:T(8,128)S(1)} %get-tuple-element.8), channel_id=1, source_target_pairs={{0,1},{1,0},{2,3},{3,2},{4,5},{5,4},{6,7},{7,6},{8,9},{9,8},{10,11... | collective-permute-start | bytes 1966088 | tf_op jit(solution)/shard_map/ppermute | solution.py:389
  14.3 1.7 %collective-permute-done = f32[16,10,8,128]{3,2,1,0:T(8,128)S(1)} collective-permute-done((f32[16,10,8,128]{3,2,1,0:T(8,128)S(1)}, f32[16,10,8,128]{3,2,1,0:T(8,128)S(1)}, u32[]{:S(2)}, u32[]{:S(2)}) %collective-permute-start) | collective-permute-done | bytes 655392 | tf_op jit(solution)/shard_map/ppermute | solution.py:389
  16.0 0.1 add.11
  16.1 17.3 %all_to_all.15 = f32[16,10,8,128]{3,2,1,0:T(8,128)S(1)} all-to-all(f32[16,10,8,128]{3,2,1,0:T(8,128)S(1)} %add.11), channel_id=1, replica_groups=mesh['rows_0'=4,'rows_1'=4,'rows_2'=8,'rows_3'=2] {'rows_0','rows_1'}, dimensions={0} | all-to-all | bytes 1310720 | tf_op jit(solution)/shard_map/all_to_all | solution.py:398
  33.4 15.6 %all_to_all.16 = f32[8,3,8,128]{3,2,1,0:T(8,128)S(1)} all-to-all(f32[8,3,8,128]{3,2,1,0:T(8,128)S(1)} %pad_maximum_fusion.1), channel_id=1, replica_groups=mesh['rows_0'=4,'rows_1'=4,'rows_2'=8,'rows_3'=2] {'rows_2'}, dimensions={0} | all-to-all | bytes 196608 | tf_op jit(solution)/shard_map/all_to_all | solution.py:401
  49.1 10.0 %all_to_all.17 = f32[16,2,8,128]{3,2,1,0:T(8,128)S(1)} all-to-all(f32[16,2,8,128]{3,2,1,0:T(8,128)S(1)} %broadcast_in_dim.8), channel_id=1, replica_groups=mesh['rows_0'=4,'rows_1'=4,'rows_2'=8,'rows_3'=2] {'rows_0','rows_1'}, dimensions={0} | all-to-all | bytes 262144 | tf_op jit(solution)/shard_map/all_to_all | solution.py:404
  59.1 4.0 %collective-permute-start.1 = (f32[33,8,128]{2,1,0:T(8,128)S(1)}, f32[33,8,128]{2,1,0:T(8,128)S(1)}, u32[]{:S(2)}, u32[]{:S(2)}) collective-permute-start(f32[33,8,128]{2,1,0:T(8,128)S(1)} %pad_maximum_fusion.mine), channel_id=1, source_target_pairs={{0,1},{1,0},{2,3},{3,2},{4,5},{5,4},{6,7},{7,6},{8,9},{9,8},{10,11... | collective-permute-start | bytes 405512 | tf_op jit(solution)/shard_map/ppermute | solution.py:389
  63.1 1.0 %collective-permute-done.1.theirs = f32[33,8,128]{2,1,0:T(8,128)S(1)} collective-permute-done((f32[33,8,128]{2,1,0:T(8,128)S(1)}, f32[33,8,128]{2,1,0:T(8,128)S(1)}, u32[]{:S(2)}, u32[]{:S(2)}) %collective-permute-start.1) | collective-permute-done | bytes 135200 | tf_op jit(solution)/shard_map/ppermute | solution.py:389
  64.1 0.0 copy-done
  64.1 10.9 %finish.1 = (f32[2,4]{1,0:T(2,128)}, f32[2,8192]{1,0:T(2,128)}) custom-call(s32[2]{0:T(128)} %chosen.3, s32[2]{0:T(128)S(1)} %pad_add_fusion.core.where, f32[33,8,128]{2,1,0:T(8,128)S(1)} %pad_maximum_fusion.mine, f32[33,8,128]{2,1,0:T(8,128)S(1)} %collective-permute-done.1.theirs, f32[8,128]{1,0:T(8,128)S(1)} %bitcast.7, ...), custom_call_target="tpu_custom_call" | custom-call | tf_op jit(solution)/shard_map/finish/pallas_call | solution.py:365
  (10 shorter events, 0.1 us)
Async XLA Ops:
  11.0 53.1 %copy-start = (f32[1024]{0:T(1024)S(1)}, f32[1024]{0:T(1024)}, u32[]{:S(2)}) copy-start(f32[1024]{0:T(1024)} %param.8) | copy-start | bytes 12292
  11.0 5.0 %collective-permute-start = (f32[16,10,8,128]{3,2,1,0:T(8,128)S(1)}, f32[16,10,8,128]{3,2,1,0:T(8,128)S(1)}, u32[]{:S(2)}, u32[]{:S(2)}) collective-permute-start(f32[16,10,8,128]{3,2,1,0:T(8,128)S(1)} %get-tuple-element.8), channel_id=1, source_target_pairs={{0,1},{1,0},{2,3},{3,2},{4,5},{5,4},{6,7},{7,6},{8,9},{9,8},{10,11... | collective-permute-start | bytes 1966088 | tf_op jit(solution)/shard_map/ppermute | solution.py:389
  59.1 5.0 %collective-permute-start.1 = (f32[33,8,128]{2,1,0:T(8,128)S(1)}, f32[33,8,128]{2,1,0:T(8,128)S(1)}, u32[]{:S(2)}, u32[]{:S(2)}) collective-permute-start(f32[33,8,128]{2,1,0:T(8,128)S(1)} %pad_maximum_fusion.mine), channel_id=1, source_target_pairs={{0,1},{1,0},{2,3},{3,2},{4,5},{5,4},{6,7},{7,6},{8,9},{9,8},{10,11... | collective-permute-start | bytes 405512 | tf_op jit(solution)/shard_map/ppermute | solution.py:389

commit v5 on v4

--- a/solution.py
+++ b/solution.py
@@ -37,7 +37,7 @@
 
 def local_kernel(
     chosen, blocks, core, fac, wts, block_row, mine, theirs, dense,
-    fwide, acc, gram, sq8, cross8, masks, wsel, pay,
+    fwide, acc, gram, sq8, cross8, masks, wsel, pay, turned,
 ):
     step = pl.program_id(0)
     wrows = wts.shape[0]
@@ -57,7 +57,7 @@
     w = wts[...]
     for h in range(2):
         fwide[h] = fac[:, LANES * h : LANES * (h + 1)].astype(jnp.float32)
-    turned = w.T
+    turned[...] = w.T
     f = fac[...]
     gram[...] += matmul(f.T, f)
     total = acc[...]
@@ -73,13 +73,13 @@
     acc[...] = total
     wf = w.astype(jnp.float32)
     sq8[...] += jnp.sum((wf * wf).reshape(wrows // 8, 8, NCAND), axis=0)
-    rows = iota((16, LANES), 0)
-    lanes = iota((16, LANES), 1)
+    place = iota((16, wrows), 0)
     picked = jnp.zeros((16, wrows), jnp.float32)
     for row, cand in ((0, first), (1, second)):
-        base = pl.multiple_of((cand // LANES) * LANES, LANES)
-        hot = jnp.where((rows == row) & (lanes == cand - base), 1.0, 0.0).astype(jnp.bfloat16)
-        picked = picked + matmul(hot, wts[:, pl.ds(base, LANES)], ((1,), (1,)))
+        base = pl.multiple_of((cand // 16) * 16, 16)
+        near = turned[pl.ds(base, 16), :].astype(jnp.float32)
+        line = jnp.sum(jnp.where(place == cand - base, near, 0.0), axis=0, keepdims=True)
+        picked = picked + jnp.where(place == row, line, 0.0)
     cross8[...] += matmul(picked.astype(jnp.bfloat16), w)[:8]
     for q in range(wrows // LANES):
         wsel[step * (wrows // LANES) + q] = picked[:8, LANES * q : LANES * (q + 1)]
@@ -150,6 +150,7 @@
                 pltpu.VMEM((NB, NCAND, LANES), jnp.bfloat16),
                 pltpu.VMEM((groups, 8, LANES), jnp.float32),
                 pltpu.VMEM((2, NYX, SLOTS, 8, LANES), jnp.float32),
+                pltpu.VMEM((NCAND, wstep), jnp.bfloat16),
             ],
         ),
         out_shape=[payload, payload, jax.ShapeDtypeStruct((groups, 8, LANES * NB), jnp.float32)],

time: 75.3 us -> 75.3 us (level)
  no operation moved by 1% of the time
where the time goes in v5:
time: 75.3 us; the launch traced here: 75.1 us
  blocking collectives  42.9 us (57%)
  Pallas kernels  21.2 us (28%)
  starting transfers between devices  7.32 us (10%)
  waiting for transfers between devices  2.72 us (4%)
    all_to_all x1, blocking collectives, per_device(): plane = jnp.sum(lax.all_to_all(pair, YX, 0, 0, tiled=True), axis=0)  17.3 us
    all_to_all x1, blocking collectives, per_device(): summed = jnp.sum(lax.all_to_all(line, 'rows_2', 0, 0, tiled=True), axis=0)  15.6 us
    pallas_call x1, Pallas kernels, finish(): pl.pallas_call(finish_kernel, grid_spec=pltpu.PrefetchScalarGridSpec(num_...  10.9 us
    pallas_call x1, Pallas kernels, local_products(): pl.pallas_call(local_kernel, grid_spec=pltpu.PrefetchScalarGridSpec(num_s...  10.3 us
    all_to_all x1, blocking collectives, per_device(): gathered = lax.all_to_all(shared, YX, 0, 0, tiled=True)  10 us
    ppermute x2, starting transfers between devices, swap_cores(): return lax.ppermute(x, 'rows_3', [(0, 1), (1, 0)])  7.32 us
    ppermute x2, waiting for transfers between devices, swap_cores(): return lax.ppermute(x, 'rows_3', [(0, 1), (1, 0)])  2.72 us
  transfers between devices with their start and end apart: 2, of which 2 were waited for; matrix products, arithmetic and copies ran while one was open for 0% of the time, Pallas kernels for 0%

profile of v5, /device:TPU:1, one launch (start us, length us, event | category | flops | bytes accessed | tf_op | source)
XLA Modules:
  0.0 75.1 jit_solution(7390759467786983842)
XLA Ops:
  0.6 0.1 pad_add_fusion.core.where
  0.7 10.3 %local.1 = (f32[16,10,8,128]{3,2,1,0:T(8,128)S(1)}, f32[16,10,8,128]{3,2,1,0:T(8,128)S(1)}, f32[16,8,512]{2,1,0:T(8,128)S(1)}) custom-call(s32[2]{0:T(128)} %chosen.3, s32[1024]{0:T(1024)} %blocks.1, s32[2]{0:T(128)S(1)} %pad_add_fusion.core.where, bf16[8192,256]{1,0:T(8,128)(2,1)} %factor.1, bf16[2048,1024]{1,0:T(8,128)(2,1)} %wts.1, s32[1,1024]{1,0:T(1,128)} %bitcast.9), custom_call_target="tpu_custom_call" | custom-call | tf_op jit(solution)/shard_map/local/pallas_call | solution.py:133
  11.0 0.0 copy-start
  11.0 3.3 %collective-permute-start = (f32[16,10,8,128]{3,2,1,0:T(8,128)S(1)}, f32[16,10,8,128]{3,2,1,0:T(8,128)S(1)}, u32[]{:S(2)}, u32[]{:S(2)}) collective-permute-start(f32[16,10,8,128]{3,2,1,0:T(8,128)S(1)} %get-tuple-element.8), channel_id=1, source_target_pairs={{0,1},{1,0},{2,3},{3,2},{4,5},{5,4},{6,7},{7,6},{8,9},{9,8},{10,11... | collective-permute-start | bytes 1966088 | tf_op jit(solution)/shard_map/ppermute | solution.py:390
  14.3 1.7 %collective-permute-done = f32[16,10,8,128]{3,2,1,0:T(8,128)S(1)} collective-permute-done((f32[16,10,8,128]{3,2,1,0:T(8,128)S(1)}, f32[16,10,8,128]{3,2,1,0:T(8,128)S(1)}, u32[]{:S(2)}, u32[]{:S(2)}) %collective-permute-start) | collective-permute-done | bytes 655392 | tf_op jit(solution)/shard_map/ppermute | solution.py:390
  16.0 0.1 add.11
  16.1 17.3 %all_to_all.15 = f32[16,10,8,128]{3,2,1,0:T(8,128)S(1)} all-to-all(f32[16,10,8,128]{3,2,1,0:T(8,128)S(1)} %add.11), channel_id=1, replica_groups=mesh['rows_0'=4,'rows_1'=4,'rows_2'=8,'rows_3'=2] {'rows_0','rows_1'}, dimensions={0} | all-to-all | bytes 1310720 | tf_op jit(solution)/shard_map/all_to_all | solution.py:399
  33.5 15.6 %all_to_all.16 = f32[8,3,8,128]{3,2,1,0:T(8,128)S(1)} all-to-all(f32[8,3,8,128]{3,2,1,0:T(8,128)S(1)} %pad_maximum_fusion.1), channel_id=1, replica_groups=mesh['rows_0'=4,'rows_1'=4,'rows_2'=8,'rows_3'=2] {'rows_2'}, dimensions={0} | all-to-all | bytes 196608 | tf_op jit(solution)/shard_map/all_to_all | solution.py:402
  49.1 10.0 %all_to_all.17 = f32[16,2,8,128]{3,2,1,0:T(8,128)S(1)} all-to-all(f32[16,2,8,128]{3,2,1,0:T(8,128)S(1)} %broadcast_in_dim.8), channel_id=1, replica_groups=mesh['rows_0'=4,'rows_1'=4,'rows_2'=8,'rows_3'=2] {'rows_0','rows_1'}, dimensions={0} | all-to-all | bytes 262144 | tf_op jit(solution)/shard_map/all_to_all | solution.py:405
  59.1 4.0 %collective-permute-start.1 = (f32[33,8,128]{2,1,0:T(8,128)S(1)}, f32[33,8,128]{2,1,0:T(8,128)S(1)}, u32[]{:S(2)}, u32[]{:S(2)}) collective-permute-start(f32[33,8,128]{2,1,0:T(8,128)S(1)} %pad_maximum_fusion.mine), channel_id=1, source_target_pairs={{0,1},{1,0},{2,3},{3,2},{4,5},{5,4},{6,7},{7,6},{8,9},{9,8},{10,11... | collective-permute-start | bytes 405512 | tf_op jit(solution)/shard_map/ppermute | solution.py:390
  63.2 1.0 %collective-permute-done.1.theirs = f32[33,8,128]{2,1,0:T(8,128)S(1)} collective-permute-done((f32[33,8,128]{2,1,0:T(8,128)S(1)}, f32[33,8,128]{2,1,0:T(8,128)S(1)}, u32[]{:S(2)}, u32[]{:S(2)}) %collective-permute-start.1) | collective-permute-done | bytes 135200 | tf_op jit(solution)/shard_map/ppermute | solution.py:390
  64.1 0.0 copy-done
  64.1 10.9 %finish.1 = (f32[2,4]{1,0:T(2,128)}, f32[2,8192]{1,0:T(2,128)}) custom-call(s32[2]{0:T(128)} %chosen.3, s32[2]{0:T(128)S(1)} %pad_add_fusion.core.where, f32[33,8,128]{2,1,0:T(8,128)S(1)} %pad_maximum_fusion.mine, f32[33,8,128]{2,1,0:T(8,128)S(1)} %collective-permute-done.1.theirs, f32[8,128]{1,0:T(8,128)S(1)} %bitcast.7, ...), custom_call_target="tpu_custom_call" | custom-call | tf_op jit(solution)/shard_map/finish/pallas_call | solution.py:366
  (10 shorter events, 0.1 us)
Async XLA Ops:
  11.0 53.1 %copy-start = (f32[1024]{0:T(1024)S(1)}, f32[1024]{0:T(1024)}, u32[]{:S(2)}) copy-start(f32[1024]{0:T(1024)} %param.8) | copy-start | bytes 12292
  11.0 5.0 %collective-permute-start = (f32[16,10,8,128]{3,2,1,0:T(8,128)S(1)}, f32[16,10,8,128]{3,2,1,0:T(8,128)S(1)}, u32[]{:S(2)}, u32[]{:S(2)}) collective-permute-start(f32[16,10,8,128]{3,2,1,0:T(8,128)S(1)} %get-tuple-element.8), channel_id=1, source_target_pairs={{0,1},{1,0},{2,3},{3,2},{4,5},{5,4},{6,7},{7,6},{8,9},{9,8},{10,11... | collective-permute-start | bytes 1966088 | tf_op jit(solution)/shard_map/ppermute | solution.py:390
  59.1 5.0 %collective-permute-start.1 = (f32[33,8,128]{2,1,0:T(8,128)S(1)}, f32[33,8,128]{2,1,0:T(8,128)S(1)}, u32[]{:S(2)}, u32[]{:S(2)}) collective-permute-start(f32[33,8,128]{2,1,0:T(8,128)S(1)} %pad_maximum_fusion.mine), channel_id=1, source_target_pairs={{0,1},{1,0},{2,3},{3,2},{4,5},{5,4},{6,7},{7,6},{8,9},{9,8},{10,11... | collective-permute-start | bytes 405512 | tf_op jit(solution)/shard_map/ppermute | solution.py:390
